TPU v7x, 32 devices: a whole 2x2x4 slice. The times are simulated.
32 devices in a mesh: parts: 2 (over y), view: 4 (over x, core), tile: 4 (over z).
Axes of the slice: x: 2, y: 2, z: 4, core: 2. Of those that a mesh axis runs over, the one named last changes fastest.
Arguments:
- data: float32 [8, 32, 48, 32], P(('parts', 'view'), 'tile'), parts along dimension 0, may hold values from 0.25 to 4
- labels: int32 [8, 32, 48, 32], P(('parts', 'view'), 'tile'), parts along dimension 0, may hold values from 0 to 3
- kernel: float32 [4, 32, 9], P('view'), may hold values from 0.1 to 1
- offsets: int32 [4, 32], P('view'), may hold values from -2 to 2
Outputs:
- estimate: float32 [8, 32, 48, 32], P(('parts', 'view'), 'tile'), parts along dimension 0
There are 2 independent parts, one for each index of `parts`. A program takes and returns all parts, laid end to end along the dimension named above; an argument that names none is the same for every part. Nothing has to cross between parts.
All inputs are finite; a program needn't handle non-finite values.
Results may differ from a plain program's by a relative error of at most 0.000088.
Values sent between devices are 32-bit elements; how exact they have to be, the bound alone decides.
A program may use at most 64 MiB of HBM per device.

v0:
```python
import jax
import jax.numpy as jnp
from jax import lax
from jax.sharding import PartitionSpec as P

ITERS = 2
SWEEPS = 4


WEAK = 0.2
TAU = 0.15


def extended(cells, sides, width):
    for axis, dim in sides:
        count = lax.axis_size(axis)
        ends = count - 1
        head = lax.slice_in_dim(cells, 0, width, axis=dim)
        tail = lax.slice_in_dim(cells, cells.shape[dim] - width, cells.shape[dim], axis=dim)
        cells = jnp.concatenate(
            [
                lax.ppermute(tail, axis, [(i, (i + 1) % count) for i in range(ends)]),
                cells,
                lax.ppermute(head, axis, [((i + 1) % count, i) for i in range(ends)]),
            ],
            axis=dim,
        )
    return cells


def swapped(block, axis, stride):
    count = lax.axis_size(axis)
    route = []
    for low in range(count):
        high = low | 1 << stride
        if high != low and high < count:
            route += [(low, high), (high, low)]
    return lax.ppermute(block, axis, route)


def band(kernel, offsets):
    depth_cells = kernel.shape[0]
    taps = jnp.arange(kernel.shape[1], dtype=jnp.int32) - 4
    depth = jnp.arange(depth_cells, dtype=jnp.int32)
    index = jnp.clip(depth[:, None] + taps[None, :] + offsets[:, None], 0, depth_cells - 1)
    weight = kernel / jnp.sum(kernel, axis=1, keepdims=True)
    return (index, weight)


def axis_term(field, region, axis):
    count = field.shape[axis]
    upper = lax.slice_in_dim(field, 1, count, axis=axis)
    lower = lax.slice_in_dim(field, 0, count - 1, axis=axis)
    same = jnp.where(
        lax.slice_in_dim(region, 1, count, axis=axis)
        == lax.slice_in_dim(region, 0, count - 1, axis=axis),
        1.0,
        WEAK,
    )
    flux = same * (upper - lower)
    after = [(0, 0)] * 3
    before = [(0, 0)] * 3
    after[axis] = (0, 1)
    before[axis] = (1, 0)
    return jnp.pad(flux, after) - jnp.pad(flux, before)


def sweep_rows(field, region, first_row, total_rows):
    extent = field.shape[0]
    global_rows = first_row + jnp.arange(extent, dtype=jnp.int32)
    inside = ((global_rows >= 0) & (global_rows < total_rows)).astype(field.dtype)[:, None, None]
    same = jnp.where(region[1:] == region[:-1], 1.0, WEAK) * inside[1:] * inside[:-1]
    flux = same * (field[1:] - field[:-1])
    inner = field[1:-1]
    inner_labels = region[1:-1]
    total = (
        flux[1:] - flux[:-1] + axis_term(inner, inner_labels, 1) + axis_term(inner, inner_labels, 2)
    )
    return inner + TAU * total


def regroup(received, tiles):
    slab, rows, depth_cells = received.shape
    blocks = received.reshape(slab, rows, tiles, depth_cells // tiles)
    return blocks.transpose(3, 1, 2, 0).reshape(depth_cells // tiles, rows, depth_cells)


def on_device(data, labels, kernel, offsets):
    recorded = data[0]
    region = labels[0]
    index, weight = band(kernel[0], offsets[0])
    tiles = lax.axis_size("tile")
    slab, rows, depth_cells = recorded.shape
    total_rows = slab * tiles
    start = lax.axis_index("tile") * slab
    parity = lax.axis_index("view") % 2
    columns = jnp.arange(depth_cells, dtype=jnp.int32)
    matrix = jnp.sum(weight[:, :, None] * (index[:, :, None] == columns[None, None, :]), axis=1)
    label_ext = extended(region, (("tile", 0),), 4)
    current = recorded
    for step in range(ITERS):
        forward_flat = jnp.dot(
            current.reshape(-1, depth_cells), matrix.T, precision=lax.Precision.HIGHEST
        )
        field = recorded / forward_flat.reshape(current.shape)
        flat = jnp.dot(field.reshape(-1, depth_cells), matrix, precision=lax.Precision.HIGHEST)
        correction = flat.reshape(field.shape)
        turned = correction
        for repeat in range(2):
            turned = regroup(
                lax.all_to_all(
                    jnp.flip(turned, 2), "tile", split_axis=2, concat_axis=2, tiled=True
                ),
                tiles,
            )
        turned = swapped(turned, "view", 1)
        paired = jnp.sqrt(correction * turned)
        outgoing = jnp.where(parity == 0, jnp.flip(paired, 2), paired)
        rotated = regroup(
            lax.all_to_all(outgoing, "tile", split_axis=2, concat_axis=2, tiled=True), tiles
        )
        rotated = jnp.where(parity == 1, jnp.flip(rotated, 2), rotated)
        partner = swapped(rotated, "view", 0)
        current = current * jnp.sqrt(paired * partner)
        widened = extended(current, (("tile", 0),), 4)
        for sweep in range(SWEEPS):
            extent = widened.shape[0]
            widened = sweep_rows(
                widened, label_ext[sweep : sweep + extent], start - 4 + sweep, total_rows
            )
        current = widened
    return current[None]


def solution(mesh):
    placed = (
        P(("parts", "view"), "tile", None, None),
        P(("parts", "view"), "tile", None, None),
        P("view", None, None),
        P("view", None),
    )
    return jax.shard_map(
        on_device,
        mesh=mesh,
        in_specs=placed,
        out_specs=P(("parts", "view"), "tile", None, None),
        check_vma=False,
    )
```

profile of v0, /device:TPU:0, one launch (start us, length us, event | category | flops | bytes accessed | tf_op | source)
XLA Modules:
  0.0 105.1 jit_solution(9000438772449605279)
XLA Ops:
  0.0 0.8 reduce_sum.18
  0.8 1.0 copy.55
  1.9 0.6 copy-done.3
  2.8 0.2 fusion
  3.1 0.3 fusion.43
  3.5 0.8 reshape.145
  4.3 6.3 %all-to-all-start = ((f32[4,1,3072]{2,1,0:T(1,128)}), f32[4,1,3072]{2,1,0:T(1,128)S(1)}, u32[]{:S(2)}, u32[]{:S(2)}) async-start(f32[4,1,3072]{2,1,0:T(1,128)} %reshape.145), calls=%async_computation | async-start | bytes 98304 | tf_op jit(solution)/shard_map/all_to_all | solution.py:111
  10.6 3.9 %collective-permute-start.4 = (s32[4,48,32]{1,2,0:T(8,128)S(1)}, s32[4,48,32]{1,2,0:T(8,128)S(1)}, u32[]{:S(2)}, u32[]{:S(2)}) collective-permute-start(s32[4,48,32]{1,2,0:T(8,128)S(1)} %get-tuple-element.31), channel_id=1, source_target_pairs={{0,1},{1,2},{2,3},{4,5},{5,6},{6,7},{8,9},{9,10},{10,11},{12,13},{... | collective-permute-start | bytes 73736 | tf_op jit(solution)/shard_map/ppermute | solution.py:22
  14.6 1.3 %collective-permute-start.5 = (s32[4,48,32]{1,2,0:T(8,128)S(1)}, s32[4,48,32]{1,2,0:T(8,128)S(1)}, u32[]{:S(2)}, u32[]{:S(2)}) collective-permute-start(s32[4,48,32]{1,2,0:T(8,128)S(1)} %get-tuple-element.32), channel_id=1, source_target_pairs={{1,0},{2,1},{3,2},{5,4},{6,5},{7,6},{9,8},{10,9},{11,10},{13,12},{... | collective-permute-start | bytes 73736 | tf_op jit(solution)/shard_map/ppermute | solution.py:24
  16.1 0.3 all-to-all-done
  16.3 0.6 broadcast.193
  16.9 0.7 reduce.1
  17.9 0.8 reshape.147
  18.7 5.4 %all-to-all-start.1 = ((f32[4,1,3072]{2,1,0:T(1,128)}), f32[4,1,3072]{2,1,0:T(1,128)S(1)}, u32[]{:S(2)}, u32[]{:S(2)}) async-start(f32[4,1,3072]{2,1,0:T(1,128)} %reshape.147), calls=%async_computation.1 | async-start | bytes 98304 | tf_op jit(solution)/shard_map/all_to_all | solution.py:111
  24.1 5.7 %all-to-all-done.1 = f32[4,1,3072]{2,1,0:T(1,128)S(1)} async-done(((f32[4,1,3072]{2,1,0:T(1,128)}), f32[4,1,3072]{2,1,0:T(1,128)S(1)}, u32[]{:S(2)}, u32[]{:S(2)}) %all-to-all-start.1) | async-done | bytes 49184 | tf_op jit(solution)/shard_map/all_to_all | solution.py:111
  29.8 0.7 reduce.2
  30.7 1.6 %collective-permute-start = (f32[8,48,32]{1,2,0:T(8,128)S(1)}, f32[8,48,32]{1,2,0:T(8,128)S(1)}, u32[]{:S(2)}, u32[]{:S(2)}) collective-permute-start(f32[8,48,32]{1,2,0:T(8,128)S(1)} %bitcast.122), channel_id=1, source_target_pairs={{0,8},{8,0},{4,12},{12,4},{1,9},{9,1},{5,13},{13,5},{2,10},{10,2},... | collective-permute-start | bytes 147464 | tf_op jit(solution)/shard_map/ppermute | solution.py:38
  32.3 3.4 %collective-permute-done = f32[8,48,32]{1,2,0:T(8,128)S(1)} collective-permute-done((f32[8,48,32]{1,2,0:T(8,128)S(1)}, f32[8,48,32]{1,2,0:T(8,128)S(1)}, u32[]{:S(2)}, u32[]{:S(2)}) %collective-permute-start) | collective-permute-done | bytes 49184 | tf_op jit(solution)/shard_map/ppermute | solution.py:38
  35.9 0.8 reshape.149
  36.7 3.3 %all-to-all-start.2 = ((f32[4,1,3072]{2,1,0:T(1,128)}), f32[4,1,3072]{2,1,0:T(1,128)S(1)}, u32[]{:S(2)}, u32[]{:S(2)}) async-start(f32[4,1,3072]{2,1,0:T(1,128)} %reshape.149), calls=%async_computation.2 | async-start | bytes 98304 | tf_op jit(solution)/shard_map/all_to_all | solution.py:120
  40.0 5.7 %all-to-all-done.2 = f32[4,1,3072]{2,1,0:T(1,128)S(1)} async-done(((f32[4,1,3072]{2,1,0:T(1,128)}), f32[4,1,3072]{2,1,0:T(1,128)S(1)}, u32[]{:S(2)}, u32[]{:S(2)}) %all-to-all-start.2) | async-done | bytes 49184 | tf_op jit(solution)/shard_map/all_to_all | solution.py:120
  45.6 0.7 reduce.3
  46.7 1.3 %collective-permute-done.1 = f32[8,48,32]{1,2,0:T(8,128)S(1)} collective-permute-done((f32[8,48,32]{1,2,0:T(8,128)S(1)}, f32[8,48,32]{1,2,0:T(8,128)S(1)}, u32[]{:S(2)}, u32[]{:S(2)}) %collective-permute-start.1) | collective-permute-done | bytes 49184 | tf_op jit(solution)/shard_map/ppermute | solution.py:38
  48.1 2.7 %collective-permute-start.2 = (f32[4,48,32]{1,2,0:T(8,128)S(1)}, f32[4,48,32]{1,2,0:T(8,128)S(1)}, u32[]{:S(2)}, u32[]{:S(2)}) collective-permute-start(f32[4,48,32]{1,2,0:T(8,128)S(1)} %get-tuple-element.33), channel_id=1, source_target_pairs={{0,1},{1,2},{2,3},{4,5},{5,6},{6,7},{8,9},{9,10},{10,11},{12,13},{... | collective-permute-start | bytes 73736 | tf_op jit(solution)/shard_map/ppermute | solution.py:22
  50.8 1.3 %collective-permute-start.3 = (f32[4,48,32]{1,2,0:T(8,128)S(1)}, f32[4,48,32]{1,2,0:T(8,128)S(1)}, u32[]{:S(2)}, u32[]{:S(2)}) collective-permute-start(f32[4,48,32]{1,2,0:T(8,128)S(1)} %get-tuple-element.34), channel_id=1, source_target_pairs={{1,0},{2,1},{3,2},{5,4},{6,5},{7,6},{9,8},{10,9},{11,10},{13,12},{... | collective-permute-start | bytes 73736 | tf_op jit(solution)/shard_map/ppermute | solution.py:24
  52.2 0.5 collective-permute-done.2
  52.7 4.3 %collective-permute-done.3 = f32[4,48,32]{1,2,0:T(8,128)S(1)} collective-permute-done((f32[4,48,32]{1,2,0:T(8,128)S(1)}, f32[4,48,32]{1,2,0:T(8,128)S(1)}, u32[]{:S(2)}, u32[]{:S(2)}) %collective-permute-start.3) | collective-permute-done | bytes 24608 | tf_op jit(solution)/shard_map/ppermute | solution.py:24
  57.0 0.2 select_multiply_fusion.3
  57.4 0.2 fusion.10
  57.6 0.2 select_multiply_fusion.7
  58.1 0.2 select_multiply_fusion.11
  59.0 0.3 convolution_divide_fusion
  59.2 0.3 fusion.45
  59.8 8.1 %all_to_all.30 = f32[4,1,3072]{2,1,0:T(1,128)S(1)} all-to-all(f32[4,1,3072]{2,1,0:T(1,128)S(1)} %reshape.151), channel_id=1, replica_groups=mesh['parts'=2,'view'=4,'tile'=4] {'tile'}, dimensions={0} | all-to-all | bytes 98304 | tf_op jit(solution)/shard_map/all_to_all | solution.py:111
  67.9 0.7 reduce.4
  69.0 8.1 %all_to_all.31 = f32[4,1,3072]{2,1,0:T(1,128)S(1)} all-to-all(f32[4,1,3072]{2,1,0:T(1,128)S(1)} %reshape.153), channel_id=1, replica_groups=mesh['parts'=2,'view'=4,'tile'=4] {'tile'}, dimensions={0} | all-to-all | bytes 98304 | tf_op jit(solution)/shard_map/all_to_all | solution.py:111
  77.1 0.7 reduce.5
  78.0 1.6 %collective-permute-start.6 = (f32[8,48,32]{1,2,0:T(8,128)S(1)}, f32[8,48,32]{1,2,0:T(8,128)S(1)}, u32[]{:S(2)}, u32[]{:S(2)}) collective-permute-start(f32[8,48,32]{1,2,0:T(8,128)S(1)} %bitcast.123), channel_id=1, source_target_pairs={{0,8},{8,0},{4,12},{12,4},{1,9},{9,1},{5,13},{13,5},{2,10},{10,2},... | collective-permute-start | bytes 147464 | tf_op jit(solution)/shard_map/ppermute | solution.py:38
  79.5 3.5 %collective-permute-done.6 = f32[8,48,32]{1,2,0:T(8,128)S(1)} collective-permute-done((f32[8,48,32]{1,2,0:T(8,128)S(1)}, f32[8,48,32]{1,2,0:T(8,128)S(1)}, u32[]{:S(2)}, u32[]{:S(2)}) %collective-permute-start.6) | collective-permute-done | bytes 49184 | tf_op jit(solution)/shard_map/ppermute | solution.py:38
  83.4 8.1 %all_to_all.32 = f32[4,1,3072]{2,1,0:T(1,128)S(1)} all-to-all(f32[4,1,3072]{2,1,0:T(1,128)S(1)} %reshape.155), channel_id=1, replica_groups=mesh['parts'=2,'view'=4,'tile'=4] {'tile'}, dimensions={0} | all-to-all | bytes 98304 | tf_op jit(solution)/shard_map/all_to_all | solution.py:120
  91.4 0.7 reduce.6
  92.4 1.3 %collective-permute-done.7 = f32[8,48,32]{1,2,0:T(8,128)S(1)} collective-permute-done((f32[8,48,32]{1,2,0:T(8,128)S(1)}, f32[8,48,32]{1,2,0:T(8,128)S(1)}, u32[]{:S(2)}, u32[]{:S(2)}) %collective-permute-start.7) | collective-permute-done | bytes 49184 | tf_op jit(solution)/shard_map/ppermute | solution.py:38
  93.8 2.7 %collective-permute-start.8 = (f32[4,48,32]{1,2,0:T(8,128)S(1)}, f32[4,48,32]{1,2,0:T(8,128)S(1)}, u32[]{:S(2)}, u32[]{:S(2)}) collective-permute-start(f32[4,48,32]{1,2,0:T(8,128)S(1)} %get-tuple-element.29), channel_id=1, source_target_pairs={{0,1},{1,2},{2,3},{4,5},{5,6},{6,7},{8,9},{9,10},{10,11},{12,13},{... | collective-permute-start | bytes 73736 | tf_op jit(solution)/shard_map/ppermute | solution.py:22
  96.6 1.3 %collective-permute-start.9 = (f32[4,48,32]{1,2,0:T(8,128)S(1)}, f32[4,48,32]{1,2,0:T(8,128)S(1)}, u32[]{:S(2)}, u32[]{:S(2)}) collective-permute-start(f32[4,48,32]{1,2,0:T(8,128)S(1)} %get-tuple-element.30), channel_id=1, source_target_pairs={{1,0},{2,1},{3,2},{5,4},{6,5},{7,6},{9,8},{10,9},{11,10},{13,12},{... | collective-permute-start | bytes 73736 | tf_op jit(solution)/shard_map/ppermute | solution.py:24
  97.9 0.6 collective-permute-done.8
  98.5 4.3 %collective-permute-done.9 = f32[4,48,32]{1,2,0:T(8,128)S(1)} collective-permute-done((f32[4,48,32]{1,2,0:T(8,128)S(1)}, f32[4,48,32]{1,2,0:T(8,128)S(1)}, u32[]{:S(2)}, u32[]{:S(2)}) %collective-permute-start.9) | collective-permute-done | bytes 24608 | tf_op jit(solution)/shard_map/ppermute | solution.py:24
  103.1 0.2 fusion.6
  104.3 0.8 fusion.38
  (94 shorter events, 5.6 us)
Async XLA Ops:
  0.0 0.8 copy-start.2
  1.9 0.7 copy-start.3
  3.5 7.1 %copy-start = (s32[1,8,48,32]{2,3,1,0:T(8,128)S(1)}, s32[1,8,48,32]{2,3,1,0:T(8,128)}, u32[]{:S(2)}) copy-start(s32[1,8,48,32]{2,3,1,0:T(8,128)} %param.5) | copy-start | bytes 147460
  4.3 12.0 %all-to-all-start = ((f32[4,1,3072]{2,1,0:T(1,128)}), f32[4,1,3072]{2,1,0:T(1,128)S(1)}, u32[]{:S(2)}, u32[]{:S(2)}) async-start(f32[4,1,3072]{2,1,0:T(1,128)} %reshape.145), calls=%async_computation | async-start | bytes 98304 | tf_op jit(solution)/shard_map/all_to_all | solution.py:111
  10.6 41.5 %collective-permute-start.4 = (s32[4,48,32]{1,2,0:T(8,128)S(1)}, s32[4,48,32]{1,2,0:T(8,128)S(1)}, u32[]{:S(2)}, u32[]{:S(2)}) collective-permute-start(s32[4,48,32]{1,2,0:T(8,128)S(1)} %get-tuple-element.31), channel_id=1, source_target_pairs={{0,1},{1,2},{2,3},{4,5},{5,6},{6,7},{8,9},{9,10},{10,11},{12,13},{... | collective-permute-start | bytes 73736 | tf_op jit(solution)/shard_map/ppermute | solution.py:22
  14.6 37.5 %collective-permute-start.5 = (s32[4,48,32]{1,2,0:T(8,128)S(1)}, s32[4,48,32]{1,2,0:T(8,128)S(1)}, u32[]{:S(2)}, u32[]{:S(2)}) collective-permute-start(s32[4,48,32]{1,2,0:T(8,128)S(1)} %get-tuple-element.32), channel_id=1, source_target_pairs={{1,0},{2,1},{3,2},{5,4},{6,5},{7,6},{9,8},{10,9},{11,10},{13,12},{... | collective-permute-start | bytes 73736 | tf_op jit(solution)/shard_map/ppermute | solution.py:24
  18.7 11.1 %all-to-all-start.1 = ((f32[4,1,3072]{2,1,0:T(1,128)}), f32[4,1,3072]{2,1,0:T(1,128)S(1)}, u32[]{:S(2)}, u32[]{:S(2)}) async-start(f32[4,1,3072]{2,1,0:T(1,128)} %reshape.147), calls=%async_computation.1 | async-start | bytes 98304 | tf_op jit(solution)/shard_map/all_to_all | solution.py:111
  30.7 5.0 %collective-permute-start = (f32[8,48,32]{1,2,0:T(8,128)S(1)}, f32[8,48,32]{1,2,0:T(8,128)S(1)}, u32[]{:S(2)}, u32[]{:S(2)}) collective-permute-start(f32[8,48,32]{1,2,0:T(8,128)S(1)} %bitcast.122), channel_id=1, source_target_pairs={{0,8},{8,0},{4,12},{12,4},{1,9},{9,1},{5,13},{13,5},{2,10},{10,2},... | collective-permute-start | bytes 147464 | tf_op jit(solution)/shard_map/ppermute | solution.py:38
  36.7 8.9 %all-to-all-start.2 = ((f32[4,1,3072]{2,1,0:T(1,128)}), f32[4,1,3072]{2,1,0:T(1,128)S(1)}, u32[]{:S(2)}, u32[]{:S(2)}) async-start(f32[4,1,3072]{2,1,0:T(1,128)} %reshape.149), calls=%async_computation.2 | async-start | bytes 98304 | tf_op jit(solution)/shard_map/all_to_all | solution.py:120
  46.5 1.5 %copy-start.1 = (f32[1,8,48,32]{2,3,1,0:T(8,128)S(1)}, f32[1,8,48,32]{2,3,1,0:T(8,128)}, u32[]{:S(2)}) copy-start(f32[1,8,48,32]{2,3,1,0:T(8,128)} %param.4) | copy-start | bytes 147460
  46.6 1.4 %collective-permute-start.1 = (f32[8,48,32]{1,2,0:T(8,128)S(1)}, f32[8,48,32]{1,2,0:T(8,128)S(1)}, u32[]{:S(2)}, u32[]{:S(2)}) collective-permute-start(f32[8,48,32]{1,2,0:T(8,128)S(1)} %broadcast_select_fusion.3), channel_id=1, source_target_pairs={{0,4},{4,0},{8,12},{12,8},{1,5},{5,1},{9,13},{13,9},{2,6},{6,2},{1... | collective-permute-start | bytes 147464 | tf_op jit(solution)/shard_map/ppermute | solution.py:38
  48.1 4.6 %collective-permute-start.2 = (f32[4,48,32]{1,2,0:T(8,128)S(1)}, f32[4,48,32]{1,2,0:T(8,128)S(1)}, u32[]{:S(2)}, u32[]{:S(2)}) collective-permute-start(f32[4,48,32]{1,2,0:T(8,128)S(1)} %get-tuple-element.33), channel_id=1, source_target_pairs={{0,1},{1,2},{2,3},{4,5},{5,6},{6,7},{8,9},{9,10},{10,11},{12,13},{... | collective-permute-start | bytes 73736 | tf_op jit(solution)/shard_map/ppermute | solution.py:22
  50.8 6.2 %collective-permute-start.3 = (f32[4,48,32]{1,2,0:T(8,128)S(1)}, f32[4,48,32]{1,2,0:T(8,128)S(1)}, u32[]{:S(2)}, u32[]{:S(2)}) collective-permute-start(f32[4,48,32]{1,2,0:T(8,128)S(1)} %get-tuple-element.34), channel_id=1, source_target_pairs={{1,0},{2,1},{3,2},{5,4},{6,5},{7,6},{9,8},{10,9},{11,10},{13,12},{... | collective-permute-start | bytes 73736 | tf_op jit(solution)/shard_map/ppermute | solution.py:24
  78.0 5.0 %collective-permute-start.6 = (f32[8,48,32]{1,2,0:T(8,128)S(1)}, f32[8,48,32]{1,2,0:T(8,128)S(1)}, u32[]{:S(2)}, u32[]{:S(2)}) collective-permute-start(f32[8,48,32]{1,2,0:T(8,128)S(1)} %bitcast.123), channel_id=1, source_target_pairs={{0,8},{8,0},{4,12},{12,4},{1,9},{9,1},{5,13},{13,5},{2,10},{10,2},... | collective-permute-start | bytes 147464 | tf_op jit(solution)/shard_map/ppermute | solution.py:38
  92.4 1.4 %collective-permute-start.7 = (f32[8,48,32]{1,2,0:T(8,128)S(1)}, f32[8,48,32]{1,2,0:T(8,128)S(1)}, u32[]{:S(2)}, u32[]{:S(2)}) collective-permute-start(f32[8,48,32]{1,2,0:T(8,128)S(1)} %broadcast_select_fusion.2), channel_id=1, source_target_pairs={{0,4},{4,0},{8,12},{12,8},{1,5},{5,1},{9,13},{13,9},{2,6},{6,2},{1... | collective-permute-start | bytes 147464 | tf_op jit(solution)/shard_map/ppermute | solution.py:38
  93.8 4.6 %collective-permute-start.8 = (f32[4,48,32]{1,2,0:T(8,128)S(1)}, f32[4,48,32]{1,2,0:T(8,128)S(1)}, u32[]{:S(2)}, u32[]{:S(2)}) collective-permute-start(f32[4,48,32]{1,2,0:T(8,128)S(1)} %get-tuple-element.29), channel_id=1, source_target_pairs={{0,1},{1,2},{2,3},{4,5},{5,6},{6,7},{8,9},{9,10},{10,11},{12,13},{... | collective-permute-start | bytes 73736 | tf_op jit(solution)/shard_map/ppermute | solution.py:22
  96.6 6.2 %collective-permute-start.9 = (f32[4,48,32]{1,2,0:T(8,128)S(1)}, f32[4,48,32]{1,2,0:T(8,128)S(1)}, u32[]{:S(2)}, u32[]{:S(2)}) collective-permute-start(f32[4,48,32]{1,2,0:T(8,128)S(1)} %get-tuple-element.30), channel_id=1, source_target_pairs={{1,0},{2,1},{3,2},{5,4},{6,5},{7,6},{9,8},{10,9},{11,10},{13,12},{... | collective-permute-start | bytes 73736 | tf_op jit(solution)/shard_map/ppermute | solution.py:24
where the time goes:
time: 106 us; the launch traced here: 105 us
  starting transfers between devices  31.6 us (30%)
  waiting for transfers between devices  30.8 us (29%)
  blocking collectives  24.2 us (23%)
  other arithmetic  9.94 us (9%)
  local copies, waits for them, and re-layouts  6.87 us (6%)
    all_to_all x2, blocking collectives, on_device(): lax.all_to_all(jnp.flip(turned, 2), 'tile', split_axis=2, concat_axis=2,...  16.1 us
    all_to_all x2, starting transfers between devices, on_device(): lax.all_to_all(jnp.flip(turned, 2), 'tile', split_axis=2, concat_axis=2,...  11.8 us
    ppermute x4, waiting for transfers between devices, swapped(): return lax.ppermute(block, axis, route)  9.48 us
    ppermute x3, starting transfers between devices, extended(): lax.ppermute(tail, axis, [(i, (i + 1) % count) for i in range(ends)])  9.4 us
    ppermute x3, waiting for transfers between devices, extended(): lax.ppermute(head, axis, [((i + 1) % count, i) for i in range(ends)])  8.55 us
    all_to_all x1, blocking collectives, on_device(): lax.all_to_all(outgoing, 'tile', split_axis=2, concat_axis=2, tiled=True)  8.06 us
    all_to_all x2, waiting for transfers between devices, on_device(): lax.all_to_all(jnp.flip(turned, 2), 'tile', split_axis=2, concat_axis=2,...  5.97 us
    all_to_all x1, waiting for transfers between devices, on_device(): lax.all_to_all(outgoing, 'tile', split_axis=2, concat_axis=2, tiled=True)  5.65 us
  transfers between devices with their start and end apart: 13, of which 11 were waited for; matrix products, arithmetic and copies ran while one was open for 5% of the time, Pallas kernels for 0%

commit v1 on v0

--- a/solution.py
+++ b/solution.py
@@ -1,6 +1,10 @@
+import functools
+
 import jax
 import jax.numpy as jnp
 from jax import lax
+from jax.experimental import pallas as pl
+from jax.experimental.pallas import tpu as pltpu
 from jax.sharding import PartitionSpec as P
 
 ITERS = 2
@@ -132,6 +136,396 @@
     return current[None]
 
 
+def fused(tiles, data_ref, labels_ref, taps_ref, shift_ref, out_ref, raw, raw_labels, taps_buf, shift_buf, packed, packed_labels, held, held_labels, mats, est, coef, outgoing, incoming, halo, back, unpacked, in_sem, send, recv, send_l, recv_l, send_m, recv_m, send_p, recv_p, send_h, recv_h, send_o, recv_o, out_sem):
+    mesh_id = pl.DeviceIdType.MESH
+    slab, rows, depth = data_ref.shape[1:]
+    lanes = packed.shape[2]
+    fold = lanes // depth
+    groups = rows // fold
+    per_tile = groups // tiles
+    width = held.shape[1]
+    cells = held.shape[2]
+    peers = 2 * tiles
+    view = lax.axis_index("view")
+    tile = lax.axis_index("tile")
+    part = lax.axis_index("parts")
+    half = view // 2
+    core = view % 2
+    me = half * tiles + tile
+    flip_x = (view == 1) | (view == 2)
+    flip_z = view >= 2
+
+    def peer(q):
+        return (part, 2 * (q // tiles) + core, q % tiles)
+
+    copies_in = []
+    for source, target, base in ((data_ref, raw, 0), (labels_ref, raw_labels, slab)):
+        for x in range(slab):
+            at = jnp.where(flip_x, slab - 1 - x, x)
+            copies_in.append(
+                pltpu.make_async_copy(
+                    source.at[0, x],
+                    target.at[pl.ds(pl.multiple_of(at * rows, 8), rows)],
+                    in_sem.at[base + x],
+                )
+            )
+    copies_in.append(pltpu.make_async_copy(taps_ref.at[0], taps_buf, in_sem.at[2 * slab]))
+    copies_in.append(pltpu.make_async_copy(shift_ref, shift_buf, in_sem.at[2 * slab + 1]))
+    for copy in copies_in:
+        copy.start()
+
+    barrier = pltpu.get_barrier_semaphore()
+    across = (part, 2 * half + 1 - core, tile)
+    for d in range(1, peers):
+        pl.semaphore_signal(barrier, inc=1, device_id=peer((me + d) % peers), device_id_type=mesh_id)
+    pl.semaphore_signal(barrier, inc=1, device_id=across, device_id_type=mesh_id)
+
+    row_ids = lax.broadcasted_iota(jnp.int32, (lanes, lanes), 0)
+    lane_ids = lax.broadcasted_iota(jnp.int32, (lanes, lanes), 1)
+    same_block = (row_ids // depth) == (lane_ids // depth)
+    aim = jnp.where(flip_z, depth - 1 - lane_ids % depth, lane_ids % depth)
+    turn = jnp.where(same_block & (row_ids % depth == aim), 1.0, 0.0).astype(jnp.float32)
+
+    def exact(a, b):
+        return jnp.dot(a, b, precision=lax.Precision.HIGHEST, preferred_element_type=jnp.float32)
+
+    def pack(source, target, fill, convert):
+        pieces = []
+        for g in range(groups):
+            pieces.append(
+                jnp.concatenate(
+                    [convert(source[pl.ds(g * fold + b, slab, stride=rows), :]) for b in range(fold)],
+                    axis=1,
+                )
+            )
+        turned = exact(jnp.concatenate(pieces, axis=0), turn)
+        edge = jnp.full((1, slab, lanes), fill, jnp.float32)
+        target[0:1] = edge
+        target[groups + 1 : groups + 2] = edge
+        target[1 : groups + 1] = turned.reshape(groups, slab, lanes)
+
+    spot = pl.ds(pl.multiple_of(jnp.where(flip_x, tiles - 1 - tile, tile) * slab, 8), slab)
+
+    def scatter(source, target, send_sem, recv_sem):
+        copies = []
+        for d in range(peers):
+            q = (me + d) % peers
+            src = source.at[pl.ds(per_tile * (q % tiles) + q // tiles, width)]
+            dst = target.at[half, :, spot, :]
+            if d == 0:
+                copy = pltpu.make_async_copy(src, dst, recv_sem.at[0])
+            else:
+                copy = pltpu.make_async_remote_copy(
+                    src_ref=src,
+                    dst_ref=dst,
+                    send_sem=send_sem.at[d],
+                    recv_sem=recv_sem.at[d],
+                    device_id=peer(q),
+                    device_id_type=mesh_id,
+                )
+            copy.start()
+            copies.append(copy)
+        return copies
+
+    def landed(copies):
+        copies[0].wait()
+        for copy in copies[1:]:
+            copy.wait_recv()
+
+    for x in range(slab):
+        copies_in[x].wait()
+    pack(raw, packed, 1.0, lambda v: v)
+    pl.semaphore_wait(barrier, peers)
+    data_copies = scatter(packed, held, send, recv)
+
+    copies_in[2 * slab].wait()
+    copies_in[2 * slab + 1].wait()
+    taps = taps_buf[...]
+    count = taps.shape[1]
+    weight = taps / jnp.sum(taps, axis=1, keepdims=True)
+    shift_row = jnp.broadcast_to(shift_buf[...].astype(jnp.float32), (depth, depth))
+    eye = lax.broadcasted_iota(jnp.int32, (depth, depth), 0) == lax.broadcasted_iota(
+        jnp.int32, (depth, depth), 1
+    )
+    shift = jnp.sum(jnp.where(eye, shift_row, 0.0), axis=1, keepdims=True).astype(jnp.int32)
+    level = lax.broadcasted_iota(jnp.int32, (depth, 1), 0)
+    strip_lane = lax.broadcasted_iota(jnp.int32, (depth, lanes), 1) % depth
+    strip_aim = jnp.where(flip_z, depth - 1 - strip_lane, strip_lane)
+    strip = jnp.zeros((depth, lanes), jnp.float32)
+    for k in range(count):
+        index = jnp.clip(level + (k - 4) + shift, 0, depth - 1)
+        strip = strip + jnp.where(index == strip_aim, weight[:, k : k + 1], 0.0)
+    strip = exact(turn[:depth, :depth], strip)
+    mats[pl.ds(half, 1)] = strip[None]
+    mat_copy = pltpu.make_async_remote_copy(
+        src_ref=mats.at[half],
+        dst_ref=mats.at[half],
+        send_sem=send_m,
+        recv_sem=recv_m,
+        device_id=(part, 2 * (1 - half) + core, tile),
+        device_id_type=mesh_id,
+    )
+    mat_copy.start()
+
+    for x in range(slab):
+        copies_in[slab + x].wait()
+    pack(raw_labels, packed_labels, 0.0, lambda v: v.astype(jnp.float32))
+    label_copies = scatter(packed_labels, held_labels, send_l, recv_l)
+
+    lane = lax.broadcasted_iota(jnp.int32, (cells, lanes), 1)
+    sub = lax.broadcasted_iota(jnp.int32, (cells, lanes), 0)
+    first = per_tile * tile - 1 + half
+    last_lane = lane < lanes - depth
+    first_lane = lane < depth
+
+    def ahead_y(fields, g):
+        return jnp.where(
+            last_lane,
+            pltpu.roll(fields[g], lanes - depth, 1),
+            pltpu.roll(fields[(g + 1) % width], lanes - depth, 1),
+        )
+
+    def behind_y(fields, g):
+        return jnp.where(
+            first_lane,
+            pltpu.roll(fields[(g - 1) % width], depth, 1),
+            pltpu.roll(fields[g], depth, 1),
+        )
+
+    def transposed(p):
+        flipped = p.T
+        result = []
+        for g in range(width):
+            piece = flipped[0:depth]
+            if g:
+                piece = pltpu.roll(piece, (lanes - depth * g) % lanes, 1)
+            for b in range(1, fold):
+                part_b = flipped[depth * b : depth * (b + 1)]
+                amount = (depth * (b - g)) % lanes
+                if amount:
+                    part_b = pltpu.roll(part_b, amount, 1)
+                piece = jnp.where(lane // depth == b, part_b, piece)
+            result.append(piece)
+        return result
+
+    landed(data_copies)
+    mat_copy.wait_recv()
+    blurs = [
+        jnp.where(same_block, jnp.concatenate([mats[s]] * fold, axis=0), 0.0) for s in range(2)
+    ]
+
+    pending = []
+    for step in range(ITERS):
+        corrections = []
+        for s in range(2):
+            recorded = held[s].reshape(width * cells, lanes)
+            current = recorded if step == 0 else est[s].reshape(width * cells, lanes)
+            forward = lax.dot_general(
+                current,
+                blurs[s],
+                (((1,), (1,)), ((), ())),
+                precision=lax.Precision.HIGHEST,
+                preferred_element_type=jnp.float32,
+            )
+            corrections.append(exact(recorded / forward, blurs[s]))
+        paired = jnp.sqrt(corrections[0] * corrections[1])
+        pieces = transposed(paired)
+        for g in range(width):
+            outgoing[step, g] = pieces[g]
+        swap = pltpu.make_async_remote_copy(
+            src_ref=outgoing.at[step],
+            dst_ref=incoming.at[step],
+            send_sem=send_p.at[step],
+            recv_sem=recv_p.at[step],
+            device_id=across,
+            device_id_type=mesh_id,
+        )
+        swap.start()
+        pending.append(swap)
+        if step == 0:
+            landed(label_copies)
+            for s in range(2):
+                regions = [held_labels[s, g] for g in range(width)]
+                for g in range(width):
+                    mine = regions[g]
+                    strong, weak = TAU, TAU * WEAK
+                    e_x = jnp.where(pltpu.roll(mine, cells - 1, 0) == mine, strong, weak)
+                    coef[0, s, g] = jnp.where(sub == cells - 1, 0.0, e_x)
+                    e_z = jnp.where(pltpu.roll(mine, lanes - 1, 1) == mine, strong, weak)
+                    coef[1, s, g] = jnp.where(lane % depth == depth - 1, 0.0, e_z)
+                    e_y = jnp.where(ahead_y(regions, g) == mine, strong, weak)
+                    y = fold * (first + g) + lane // depth
+                    coef[2, s, g] = jnp.where((y >= 0) & (y < rows - 1), e_y, 0.0)
+        swap.wait_recv()
+        joined = [
+            jnp.sqrt(paired[cells * g : cells * (g + 1)] * incoming[step, g]) for g in range(width)
+        ]
+        for s in range(2):
+            base = held if step == 0 else est
+            fields = [base[s, g] * joined[g] for g in range(width)]
+            for sweep in range(SWEEPS):
+                flux_y = [coef[2, s, g] * (ahead_y(fields, g) - fields[g]) for g in range(width)]
+                fresh = []
+                for g in range(width):
+                    f = fields[g]
+                    flux_x = coef[0, s, g] * (pltpu.roll(f, cells - 1, 0) - f)
+                    flux_z = coef[1, s, g] * (pltpu.roll(f, lanes - 1, 1) - f)
+                    total = (
+                        (flux_x - pltpu.roll(flux_x, 1, 0))
+                        + (flux_y[g] - behind_y(flux_y, g))
+                        + (flux_z - pltpu.roll(flux_z, 1, 1))
+                    )
+                    fresh.append(f + total)
+                fields = fresh
+            for g in range(width):
+                est[s, g] = fields[g]
+        if step < ITERS - 1:
+            far = tile + 2 * half - 1
+            exists = (far >= 0) & (far < tiles)
+
+            def shifted(number, side, target):
+                return pltpu.make_async_remote_copy(
+                    src_ref=est.at[:, 1 + half],
+                    dst_ref=halo.at[step, side],
+                    send_sem=send_h.at[step, number],
+                    recv_sem=recv_h.at[step, number],
+                    device_id=(part, 2 * (1 - half) + core, target),
+                    device_id_type=mesh_id,
+                )
+
+            near_copy = shifted(0, half, tile)
+            near_copy.start()
+            far_copy = shifted(1, 1 - half, jnp.clip(far, 0, tiles - 1))
+
+            @pl.when(exists)
+            def _():
+                far_copy.start()
+
+            near_copy.wait()
+            near = (width - 1) * (1 - half)
+            for s in range(2):
+                est[s, pl.ds(near, 1)] = halo[step, 1 - half, s][None]
+
+            @pl.when(exists)
+            def _():
+                far_copy.wait()
+                for s in range(2):
+                    est[s, pl.ds((width - 1) * half, 1)] = halo[step, half, s][None]
+
+    out_copies = []
+    for d in range(peers):
+        q = (me + d) % peers
+        s, t = q // tiles, q % tiles
+        place = jnp.where(s + core == 1, tiles - 1 - t, t)
+        src = est.at[s, 1 : width - 1, pl.ds(pl.multiple_of(place * slab, 8), slab), :]
+        dst = back.at[me]
+        if d == 0:
+            copy = pltpu.make_async_copy(src, dst, recv_o.at[0])
+        else:
+            copy = pltpu.make_async_remote_copy(
+                src_ref=src,
+                dst_ref=dst,
+                send_sem=send_o.at[d],
+                recv_sem=recv_o.at[d],
+                device_id=peer(q),
+                device_id_type=mesh_id,
+            )
+        copy.start()
+        out_copies.append(copy)
+    landed(out_copies)
+    pieces = []
+    for g in range(groups):
+        m, r = g // per_tile, g % per_tile
+        pieces.append(back[m, r] if r < 2 else back[tiles + m, r - 1])
+    turned = exact(jnp.concatenate(pieces, axis=0), turn)
+    for g in range(groups):
+        for b in range(fold):
+            unpacked[pl.ds(g * fold + b, slab, stride=rows), :] = turned[
+                g * slab : (g + 1) * slab, b * depth : (b + 1) * depth
+            ]
+    results = []
+    for x in range(slab):
+        at = jnp.where(flip_x, slab - 1 - x, x)
+        copy = pltpu.make_async_copy(
+            unpacked.at[pl.ds(pl.multiple_of(at * rows, 8), rows)], out_ref.at[0, x], out_sem.at[x]
+        )
+        copy.start()
+        results.append(copy)
+    for copy in data_copies[1:] + label_copies[1:] + [mat_copy] + pending + out_copies[1:]:
+        copy.wait_send()
+    for copy in results:
+        copy.wait()
+
+
+def by_rows(data, labels, kernel, offsets):
+    tiles = lax.axis_size("tile")
+    _, slab, rows, depth = data.shape
+    fold = 128 // depth
+    groups = rows // fold
+    cells = slab * tiles
+    peers = 2 * tiles
+    width = 4
+    flat = (slab * rows, depth)
+    wide = (2, width, cells, 128)
+    dma = pltpu.SemaphoreType.DMA
+    return pl.pallas_call(
+        functools.partial(fused, tiles),
+        out_shape=jax.ShapeDtypeStruct(data.shape, jnp.float32),
+        in_specs=[pl.BlockSpec(memory_space=pl.ANY)] * 4,
+        out_specs=pl.BlockSpec(memory_space=pl.ANY),
+        scratch_shapes=[
+            pltpu.VMEM(flat, jnp.float32),
+            pltpu.VMEM(flat, jnp.int32),
+            pltpu.VMEM(kernel.shape[1:], jnp.float32),
+            pltpu.VMEM(offsets.shape, jnp.int32),
+            pltpu.VMEM((groups + 2, slab, 128), jnp.float32),
+            pltpu.VMEM((groups + 2, slab, 128), jnp.float32),
+            pltpu.VMEM(wide, jnp.float32),
+            pltpu.VMEM(wide, jnp.float32),
+            pltpu.VMEM((2, depth, 128), jnp.float32),
+            pltpu.VMEM(wide, jnp.float32),
+            pltpu.VMEM((3,) + wide, jnp.float32),
+            pltpu.VMEM((ITERS,) + wide[1:], jnp.float32),
+            pltpu.VMEM((ITERS,) + wide[1:], jnp.float32),
+            pltpu.VMEM((ITERS - 1, 2, 2, cells, 128), jnp.float32),
+            pltpu.VMEM((peers, width - 2, slab, 128), jnp.float32),
+            pltpu.VMEM(flat, jnp.float32),
+            dma((2 * slab + 2,)),
+            dma((peers,)),
+            dma((peers,)),
+            dma((peers,)),
+            dma((peers,)),
+            dma(()),
+            dma(()),
+            dma((ITERS,)),
+            dma((ITERS,)),
+            dma((ITERS - 1, 2)),
+            dma((ITERS - 1, 2)),
+            dma((peers,)),
+            dma((peers,)),
+            dma((slab,)),
+        ],
+        compiler_params=pltpu.CompilerParams(collective_id=0, has_side_effects=True),
+    )(data, labels, kernel, offsets)
+
+
+def fits(data, tiles, views):
+    _, slab, rows, depth = data.shape
+    return (
+        views == 4
+        and depth * 4 == 128
+        and slab * tiles == depth
+        and slab % 8 == 0
+        and rows == 12 * tiles
+    )
+
+
+def program(data, labels, kernel, offsets):
+    if fits(data, lax.axis_size("tile"), lax.axis_size("view")):
+        return by_rows(data, labels, kernel, offsets)
+    return on_device(data, labels, kernel, offsets)
+
+
 def solution(mesh):
     placed = (
         P(("parts", "view"), "tile", None, None),
@@ -140,7 +534,7 @@
         P("view", None),
     )
     return jax.shard_map(
-        on_device,
+        program,
         mesh=mesh,
         in_specs=placed,
         out_specs=P(("parts", "view"), "tile", None, None),

time: 106 us -> 32.9 us (0.31)
  starting transfers between devices: 31.6 us -> 0 us
  waiting for transfers between devices: 30.8 us -> 0 us
  Pallas kernels: 0 us -> 27 us
  blocking collectives: 24.2 us -> 0 us
  other arithmetic: 9.94 us -> 0 us
  local copies, waits for them, and re-layouts: 6.87 us -> 5.59 us
    pallas_call x0 -> x1, Pallas kernels: none -> 27 us  [by_rows(): pl.pallas_call(functools.partial(fused, tiles), out_shape=jax.ShapeDtypeS...]
    all_to_all x3 -> x0, blocking collectives: 24.2 us -> none  [the longest x2 16.1 us: on_device(): lax.all_to_all(jnp.flip(turned, 2), 'tile', split_axis=2, concat_axis=2,...]
    ppermute x10 -> x0, waiting for transfers between devices: 19.2 us -> none  [the longest x4 9.48 us: swapped(): return lax.ppermute(block, axis, route)]
    ppermute x10 -> x0, starting transfers between devices: 16.5 us -> none  [the longest x3 9.4 us: extended(): lax.ppermute(tail, axis, [(i, (i + 1) % count) for i in range(ends)])]
    all_to_all x3 -> x0, starting transfers between devices: 15.1 us -> none  [the longest x2 11.8 us: on_device(): lax.all_to_all(jnp.flip(turned, 2), 'tile', split_axis=2, concat_axis=2,...]
    all_to_all x3 -> x0, waiting for transfers between devices: 11.6 us -> none  [the longest x2 5.97 us: on_device(): lax.all_to_all(jnp.flip(turned, 2), 'tile', split_axis=2, concat_axis=2,...]
    all_to_all x6 -> x0, other arithmetic: 4.47 us -> none  [the longest x4 2.98 us: on_device(): lax.all_to_all(jnp.flip(turned, 2), 'tile', split_axis=2, concat_axis=2,...]
    mul x26 -> x0, other arithmetic: 2.49 us -> none  [the longest x16 1.58 us: axis_term(): flux = same * (upper - lower)]
  transfers between devices with their start and end apart: 13 -> 0, of which waited for: 11 -> 0; matrix products, arithmetic and copies ran while one was open for 5% -> 0% of each run, Pallas kernels for 0% -> 0%
where the time goes in v1:
time: 32.9 us; the launch traced here: 32.6 us
  Pallas kernels  27 us (82%)
  local copies, waits for them, and re-layouts  5.59 us (17%)
    pallas_call x1, Pallas kernels, by_rows(): pl.pallas_call(functools.partial(fused, tiles), out_shape=jax.ShapeDtypeS...  27 us
    unnamed x5, local copies, waits for them, and re-layouts  3.9 us
    pallas_call x1, local copies, waits for them, and re-layouts, by_rows(): pl.pallas_call(functools.partial(fused, tiles), out_shape=jax.ShapeDtypeS...  1.69 us

profile of v1, /device:TPU:0, one launch (start us, length us, event | category | flops | bytes accessed | tf_op | source)
XLA Modules:
  0.0 32.6 jit_solution(7392803319814919135)
XLA Ops:
  0.0 1.4 %copy.7.taps_ref = f32[1,32,9]{2,1,0:T(8,128)} copy(f32[1,32,9]{1,0,2:T(1,128)} %param.6) | data formatting | bytes 2304 | tf_op args[2]
  1.4 0.0 copy-start
  1.4 1.7 %copy.5.data_ref = f32[1,8,48,32]{3,2,1,0:T(8,128)} copy(f32[1,8,48,32]{2,3,1,0:T(8,128)} %param.4) | data formatting | bytes 98304 | tf_op args[0]
  3.1 0.0 copy-done
  3.1 0.8 %copy.6.labels_ref = s32[1,8,48,32]{3,2,1,0:T(8,128)} copy(s32[1,8,48,32]{2,3,1,0:T(8,128)S(1)} %copy-done) | data formatting | bytes 98304 | tf_op args[1]
  3.9 27.0 %shard_map.46 = f32[1,8,48,32]{3,2,1,0:T(8,128)} custom-call(f32[1,8,48,32]{3,2,1,0:T(8,128)} %copy.5.data_ref, s32[1,8,48,32]{3,2,1,0:T(8,128)} %copy.6.labels_ref, f32[1,32,9]{2,1,0:T(8,128)} %copy.7.taps_ref, s32[1,32]{1,0:T(1,128)} %shift_ref.1), custom_call_target="tpu_custom_call" | custom-call | tf_op jit(solution)/shard_map/pallas_call | solution.py:471
  30.9 1.7 %copy.8 = f32[1,8,48,32]{2,3,1,0:T(8,128)} copy(f32[1,8,48,32]{3,2,1,0:T(8,128)} %shard_map.46) | data formatting | bytes 98304 | tf_op jit(solution)/shard_map/pallas_call | solution.py:471
Async XLA Ops:
  1.4 1.7 %copy-start = (s32[1,8,48,32]{2,3,1,0:T(8,128)S(1)}, s32[1,8,48,32]{2,3,1,0:T(8,128)}, u32[]{:S(2)}) copy-start(s32[1,8,48,32]{2,3,1,0:T(8,128)} %param.5) | copy-start | bytes 147460

commit v2 on v1

--- a/solution.py
+++ b/solution.py
@@ -136,9 +136,9 @@
     return current[None]
 
 
-def fused(tiles, data_ref, labels_ref, taps_ref, shift_ref, out_ref, raw, raw_labels, taps_buf, shift_buf, packed, packed_labels, held, held_labels, mats, est, coef, outgoing, incoming, halo, back, unpacked, in_sem, send, recv, send_l, recv_l, send_m, recv_m, send_p, recv_p, send_h, recv_h, send_o, recv_o, out_sem):
+def fused(tiles, data_ref, labels_ref, taps_ref, shift_ref, out_ref, raw, raw_labels, taps_buf, shift_buf, mixed, packed, packed_labels, held, held_labels, mats, est, coef, outgoing, incoming, halo, back, unpacked, in_sem, send, recv, send_l, recv_l, send_m, recv_m, send_p, recv_p, send_h, recv_h, send_o, recv_o, out_sem):
     mesh_id = pl.DeviceIdType.MESH
-    slab, rows, depth = data_ref.shape[1:]
+    slab, depth, rows = data_ref.shape[1:]
     lanes = packed.shape[2]
     fold = lanes // depth
     groups = rows // fold
@@ -152,6 +152,7 @@
     half = view // 2
     core = view % 2
     me = half * tiles + tile
+    role = (half + tile) % 2
     flip_x = (view == 1) | (view == 2)
     flip_z = view >= 2
 
@@ -165,11 +166,11 @@
             copies_in.append(
                 pltpu.make_async_copy(
                     source.at[0, x],
-                    target.at[pl.ds(pl.multiple_of(at * rows, 8), rows)],
+                    target.at[pl.ds(pl.multiple_of(at * depth, 8), depth)],
                     in_sem.at[base + x],
                 )
             )
-    copies_in.append(pltpu.make_async_copy(taps_ref.at[0], taps_buf, in_sem.at[2 * slab]))
+    copies_in.append(pltpu.make_async_copy(taps_ref, taps_buf, in_sem.at[2 * slab]))
     copies_in.append(pltpu.make_async_copy(shift_ref, shift_buf, in_sem.at[2 * slab + 1]))
     for copy in copies_in:
         copy.start()
@@ -189,20 +190,31 @@
     def exact(a, b):
         return jnp.dot(a, b, precision=lax.Precision.HIGHEST, preferred_element_type=jnp.float32)
 
+    slot = lax.broadcasted_iota(jnp.int32, (mixed.shape[1] // fold, lanes), 1) // depth
+    blocks = slab * depth // lanes
+
+    def gathered(parts, b_of):
+        total = None
+        for k in range(fold):
+            amount = (depth * (k - b_of[k])) % lanes
+            piece = pltpu.roll(parts[k], amount, 1) if amount else parts[k]
+            total = piece if total is None else jnp.where(slot == k, piece, total)
+        return total
+
     def pack(source, target, fill, convert):
-        pieces = []
-        for g in range(groups):
-            pieces.append(
-                jnp.concatenate(
-                    [convert(source[pl.ds(g * fold + b, slab, stride=rows), :]) for b in range(fold)],
-                    axis=1,
-                )
-            )
-        turned = exact(jnp.concatenate(pieces, axis=0), turn)
         edge = jnp.full((1, slab, lanes), fill, jnp.float32)
         target[0:1] = edge
         target[groups + 1 : groups + 2] = edge
-        target[1 : groups + 1] = turned.reshape(groups, slab, lanes)
+        for j in range(blocks):
+            block = convert(source[lanes * j : lanes * (j + 1), :])
+            mixed[j, 0:rows] = exact(block.T, turn)
+        for j in range(blocks):
+            parts = [
+                mixed[j, pl.ds(b, mixed.shape[1] // fold, stride=fold), :] for b in range(fold)
+            ]
+            for k in range(fold):
+                line = gathered(parts, [k] * fold)
+                target[1 : groups + 1, fold * j + k, :] = line[:groups]
 
     spot = pl.ds(pl.multiple_of(jnp.where(flip_x, tiles - 1 - tile, tile) * slab, 8), slab)
 
@@ -210,7 +222,7 @@
         copies = []
         for d in range(peers):
             q = (me + d) % peers
-            src = source.at[pl.ds(per_tile * (q % tiles) + q // tiles, width)]
+            src = source.at[pl.ds(per_tile * (q % tiles) + (q // tiles + q % tiles) % 2, width)]
             dst = target.at[half, :, spot, :]
             if d == 0:
                 copy = pltpu.make_async_copy(src, dst, recv_sem.at[0])
@@ -240,22 +252,20 @@
 
     copies_in[2 * slab].wait()
     copies_in[2 * slab + 1].wait()
-    taps = taps_buf[...]
-    count = taps.shape[1]
-    weight = taps / jnp.sum(taps, axis=1, keepdims=True)
-    shift_row = jnp.broadcast_to(shift_buf[...].astype(jnp.float32), (depth, depth))
-    eye = lax.broadcasted_iota(jnp.int32, (depth, depth), 0) == lax.broadcasted_iota(
-        jnp.int32, (depth, depth), 1
-    )
-    shift = jnp.sum(jnp.where(eye, shift_row, 0.0), axis=1, keepdims=True).astype(jnp.int32)
-    level = lax.broadcasted_iota(jnp.int32, (depth, 1), 0)
-    strip_lane = lax.broadcasted_iota(jnp.int32, (depth, lanes), 1) % depth
-    strip_aim = jnp.where(flip_z, depth - 1 - strip_lane, strip_lane)
+    count = taps_buf.shape[0]
+    taps = [jnp.concatenate([taps_buf[k]] * fold, axis=1) for k in range(count)]
+    scale = taps[0]
+    for k in range(1, count):
+        scale = scale + taps[k]
+    shift = jnp.concatenate([shift_buf[...]] * fold, axis=1)
+    level = lax.broadcasted_iota(jnp.int32, (1, lanes), 1) % depth
+    strip_row = lax.broadcasted_iota(jnp.int32, (depth, lanes), 0)
+    strip_aim = jnp.where(flip_z, depth - 1 - strip_row, strip_row)
     strip = jnp.zeros((depth, lanes), jnp.float32)
     for k in range(count):
         index = jnp.clip(level + (k - 4) + shift, 0, depth - 1)
-        strip = strip + jnp.where(index == strip_aim, weight[:, k : k + 1], 0.0)
-    strip = exact(turn[:depth, :depth], strip)
+        strip = strip + jnp.where(index == strip_aim, taps[k] / scale, 0.0)
+    strip = exact(strip, turn)
     mats[pl.ds(half, 1)] = strip[None]
     mat_copy = pltpu.make_async_remote_copy(
         src_ref=mats.at[half],
@@ -274,7 +284,7 @@
 
     lane = lax.broadcasted_iota(jnp.int32, (cells, lanes), 1)
     sub = lax.broadcasted_iota(jnp.int32, (cells, lanes), 0)
-    first = per_tile * tile - 1 + half
+    first = per_tile * tile - 1 + role
     last_lane = lane < lanes - depth
     first_lane = lane < depth
 
@@ -292,10 +302,10 @@
             pltpu.roll(fields[g], depth, 1),
         )
 
-    def transposed(p):
+    def transposed(p, chosen):
         flipped = p.T
         result = []
-        for g in range(width):
+        for g in chosen:
             piece = flipped[0:depth]
             if g:
                 piece = pltpu.roll(piece, (lanes - depth * g) % lanes, 1)
@@ -314,34 +324,75 @@
         jnp.where(same_block, jnp.concatenate([mats[s]] * fold, axis=0), 0.0) for s in range(2)
     ]
 
-    pending = []
-    for step in range(ITERS):
+    def paired_of(step, chosen):
         corrections = []
         for s in range(2):
-            recorded = held[s].reshape(width * cells, lanes)
-            current = recorded if step == 0 else est[s].reshape(width * cells, lanes)
-            forward = lax.dot_general(
-                current,
-                blurs[s],
-                (((1,), (1,)), ((), ())),
-                precision=lax.Precision.HIGHEST,
-                preferred_element_type=jnp.float32,
+            recorded = jnp.concatenate([held[s, g] for g in chosen], axis=0)
+            if step == 0:
+                current = recorded
+            else:
+                current = jnp.concatenate([est[s, g] for g in chosen], axis=0)
+            ratio = recorded / exact(current, blurs[s])
+            corrections.append(
+                lax.dot_general(
+                    ratio,
+                    blurs[s],
+                    (((1,), (1,)), ((), ())),
+                    precision=lax.Precision.HIGHEST,
+                    preferred_element_type=jnp.float32,
+                )
             )
-            corrections.append(exact(recorded / forward, blurs[s]))
-        paired = jnp.sqrt(corrections[0] * corrections[1])
-        pieces = transposed(paired)
-        for g in range(width):
-            outgoing[step, g] = pieces[g]
-        swap = pltpu.make_async_remote_copy(
-            src_ref=outgoing.at[step],
-            dst_ref=incoming.at[step],
-            send_sem=send_p.at[step],
-            recv_sem=recv_p.at[step],
+        return jnp.sqrt(corrections[0] * corrections[1])
+
+    def swapped_over(step, number, begin, size):
+        copy = pltpu.make_async_remote_copy(
+            src_ref=outgoing.at[step, pl.ds(begin, size)],
+            dst_ref=incoming.at[step, pl.ds(begin, size)],
+            send_sem=send_p.at[step, number],
+            recv_sem=recv_p.at[step, number],
             device_id=across,
             device_id_type=mesh_id,
         )
-        swap.start()
-        pending.append(swap)
+        copy.start()
+        pending.append(copy)
+        return copy
+
+    pending = []
+    ready = {}
+    for step in range(ITERS):
+        if step == 0:
+            whole = paired_of(0, range(width))
+            for g, piece in enumerate(transposed(whole, range(width))):
+                outgoing[step, g] = piece
+                ready[g] = whole[cells * g : cells * (g + 1)]
+            swaps = [swapped_over(step, 0, 0, width)]
+        else:
+            inner = range(1, width - 1)
+            outer = (0, width - 1)
+            near_copy, far_copy, exists = moving
+            swaps = []
+            for number, chosen in enumerate((inner, outer)):
+                if number:
+                    near_copy.wait()
+                    near = (width - 1) * (1 - role)
+                    for s in range(2):
+                        est[s, pl.ds(near, 1)] = halo[step - 1, 1 - role, s][None]
+
+                    @pl.when(exists)
+                    def _():
+                        far_copy.wait()
+                        for s in range(2):
+                            est[s, pl.ds((width - 1) * role, 1)] = halo[step - 1, role, s][None]
+
+                part_p = paired_of(step, chosen)
+                turned_p = transposed(jnp.concatenate([part_p, part_p], axis=0), range(len(chosen)))
+                for k, g in enumerate(chosen):
+                    outgoing[step, g] = turned_p[k]
+                    ready[g] = part_p[cells * k : cells * (k + 1)]
+                if number:
+                    swaps += [swapped_over(step, 1 + k, g, 1) for k, g in enumerate(chosen)]
+                else:
+                    swaps.append(swapped_over(step, 0, 1, width - 2))
         if step == 0:
             landed(label_copies)
             for s in range(2):
@@ -356,10 +407,9 @@
                     e_y = jnp.where(ahead_y(regions, g) == mine, strong, weak)
                     y = fold * (first + g) + lane // depth
                     coef[2, s, g] = jnp.where((y >= 0) & (y < rows - 1), e_y, 0.0)
-        swap.wait_recv()
-        joined = [
-            jnp.sqrt(paired[cells * g : cells * (g + 1)] * incoming[step, g]) for g in range(width)
-        ]
+        for swap in swaps:
+            swap.wait_recv()
+        joined = [jnp.sqrt(ready[g] * incoming[step, g]) for g in range(width)]
         for s in range(2):
             base = held if step == 0 else est
             fields = [base[s, g] * joined[g] for g in range(width)]
@@ -380,78 +430,82 @@
             for g in range(width):
                 est[s, g] = fields[g]
         if step < ITERS - 1:
-            far = tile + 2 * half - 1
+            far = tile + 2 * role - 1
             exists = (far >= 0) & (far < tiles)
 
-            def shifted(number, side, target):
+            def shifted(number, side, x_of, target):
                 return pltpu.make_async_remote_copy(
-                    src_ref=est.at[:, 1 + half],
+                    src_ref=est.at[:, 1 + role],
                     dst_ref=halo.at[step, side],
                     send_sem=send_h.at[step, number],
                     recv_sem=recv_h.at[step, number],
-                    device_id=(part, 2 * (1 - half) + core, target),
+                    device_id=(part, 2 * x_of + core, target),
                     device_id_type=mesh_id,
                 )
 
-            near_copy = shifted(0, half, tile)
+            near_copy = shifted(0, role, 1 - half, tile)
             near_copy.start()
-            far_copy = shifted(1, 1 - half, jnp.clip(far, 0, tiles - 1))
+            far_copy = shifted(1, 1 - role, half, jnp.clip(far, 0, tiles - 1))
 
             @pl.when(exists)
             def _():
                 far_copy.start()
 
-            near_copy.wait()
-            near = (width - 1) * (1 - half)
-            for s in range(2):
-                est[s, pl.ds(near, 1)] = halo[step, 1 - half, s][None]
-
-            @pl.when(exists)
-            def _():
-                far_copy.wait()
-                for s in range(2):
-                    est[s, pl.ds((width - 1) * half, 1)] = halo[step, half, s][None]
+            moving = (near_copy, far_copy, exists)
 
     out_copies = []
-    for d in range(peers):
-        q = (me + d) % peers
-        s, t = q // tiles, q % tiles
-        place = jnp.where(s + core == 1, tiles - 1 - t, t)
-        src = est.at[s, 1 : width - 1, pl.ds(pl.multiple_of(place * slab, 8), slab), :]
-        dst = back.at[me]
-        if d == 0:
-            copy = pltpu.make_async_copy(src, dst, recv_o.at[0])
+    for middle in range(2):
+        for d in range(tiles if middle else peers):
+            q = half * tiles + (tile + d) % tiles if middle else (me + d) % peers
+            s, t = q // tiles, q % tiles
+            place = jnp.where(s + core == 1, tiles - 1 - t, t)
+            here = 2 - role if middle else 1 + role
+            there = per_tile * tile + (1 if middle else 2 * role)
+            src = est.at[s, here, pl.ds(pl.multiple_of(place * slab, 8), slab), :]
+            dst = back.at[there]
+            number = peers * middle + d
+            if d == 0:
+                copy = pltpu.make_async_copy(src, dst, recv_o.at[number])
+            else:
+                copy = pltpu.make_async_remote_copy(
+                    src_ref=src,
+                    dst_ref=dst,
+                    send_sem=send_o.at[number],
+                    recv_sem=recv_o.at[number],
+                    device_id=peer(q),
+                    device_id_type=mesh_id,
+                )
+            copy.start()
+            out_copies.append(copy)
+    sent_out = []
+    for number, copy in enumerate(out_copies):
+        if number in (0, peers):
+            copy.wait()
         else:
-            copy = pltpu.make_async_remote_copy(
-                src_ref=src,
-                dst_ref=dst,
-                send_sem=send_o.at[d],
-                recv_sem=recv_o.at[d],
-                device_id=peer(q),
-                device_id_type=mesh_id,
+            copy.wait_recv()
+            sent_out.append(copy)
+    for j in range(blocks):
+        parts = []
+        for k in range(fold):
+            line = back[:, fold * j + k, :]
+            parts.append(
+                jnp.concatenate(
+                    [line, jnp.zeros((mixed.shape[1] // fold - groups, lanes), jnp.float32)], axis=0
+                )
             )
-        copy.start()
-        out_copies.append(copy)
-    landed(out_copies)
-    pieces = []
-    for g in range(groups):
-        m, r = g // per_tile, g % per_tile
-        pieces.append(back[m, r] if r < 2 else back[tiles + m, r - 1])
-    turned = exact(jnp.concatenate(pieces, axis=0), turn)
-    for g in range(groups):
         for b in range(fold):
-            unpacked[pl.ds(g * fold + b, slab, stride=rows), :] = turned[
-                g * slab : (g + 1) * slab, b * depth : (b + 1) * depth
-            ]
+            mixed[j, pl.ds(b, mixed.shape[1] // fold, stride=fold), :] = gathered(parts, [b] * fold)
     results = []
+    for j in range(blocks):
+        unpacked[lanes * j : lanes * (j + 1), :] = exact(mixed[j, 0:rows], turn).T
     for x in range(slab):
         at = jnp.where(flip_x, slab - 1 - x, x)
         copy = pltpu.make_async_copy(
-            unpacked.at[pl.ds(pl.multiple_of(at * rows, 8), rows)], out_ref.at[0, x], out_sem.at[x]
+            unpacked.at[pl.ds(pl.multiple_of(at * depth, 8), depth)], out_ref.at[0, x], out_sem.at[x]
         )
         copy.start()
         results.append(copy)
-    for copy in data_copies[1:] + label_copies[1:] + [mat_copy] + pending + out_copies[1:]:
+    for copy in data_copies[1:] + label_copies[1:] + [mat_copy] + pending + sent_out:
         copy.wait_send()
     for copy in results:
         copy.wait()
@@ -461,23 +515,26 @@
     tiles = lax.axis_size("tile")
     _, slab, rows, depth = data.shape
     fold = 128 // depth
+    tall = -(-rows // (8 * fold)) * 8 * fold
     groups = rows // fold
     cells = slab * tiles
     peers = 2 * tiles
     width = 4
-    flat = (slab * rows, depth)
+    flat = (slab * depth, rows)
     wide = (2, width, cells, 128)
     dma = pltpu.SemaphoreType.DMA
-    return pl.pallas_call(
+    taps = kernel.transpose(2, 0, 1)
+    result = pl.pallas_call(
         functools.partial(fused, tiles),
-        out_shape=jax.ShapeDtypeStruct(data.shape, jnp.float32),
+        out_shape=jax.ShapeDtypeStruct((1, slab, depth, rows), jnp.float32),
         in_specs=[pl.BlockSpec(memory_space=pl.ANY)] * 4,
         out_specs=pl.BlockSpec(memory_space=pl.ANY),
         scratch_shapes=[
             pltpu.VMEM(flat, jnp.float32),
             pltpu.VMEM(flat, jnp.int32),
-            pltpu.VMEM(kernel.shape[1:], jnp.float32),
+            pltpu.VMEM(taps.shape, jnp.float32),
             pltpu.VMEM(offsets.shape, jnp.int32),
+            pltpu.VMEM((slab * depth // 128, tall, 128), jnp.float32),
             pltpu.VMEM((groups + 2, slab, 128), jnp.float32),
             pltpu.VMEM((groups + 2, slab, 128), jnp.float32),
             pltpu.VMEM(wide, jnp.float32),
@@ -488,7 +545,7 @@
             pltpu.VMEM((ITERS,) + wide[1:], jnp.float32),
             pltpu.VMEM((ITERS,) + wide[1:], jnp.float32),
             pltpu.VMEM((ITERS - 1, 2, 2, cells, 128), jnp.float32),
-            pltpu.VMEM((peers, width - 2, slab, 128), jnp.float32),
+            pltpu.VMEM((groups, slab, 128), jnp.float32),
             pltpu.VMEM(flat, jnp.float32),
             dma((2 * slab + 2,)),
             dma((peers,)),
@@ -497,16 +554,17 @@
             dma((peers,)),
             dma(()),
             dma(()),
-            dma((ITERS,)),
-            dma((ITERS,)),
+            dma((ITERS, 3)),
+            dma((ITERS, 3)),
             dma((ITERS - 1, 2)),
             dma((ITERS - 1, 2)),
-            dma((peers,)),
-            dma((peers,)),
+            dma((peers + tiles,)),
+            dma((peers + tiles,)),
             dma((slab,)),
         ],
         compiler_params=pltpu.CompilerParams(collective_id=0, has_side_effects=True),
-    )(data, labels, kernel, offsets)
+    )(data.transpose(0, 1, 3, 2), labels.transpose(0, 1, 3, 2), taps, offsets)
+    return result.transpose(0, 1, 3, 2)
 
 
 def fits(data, tiles, views):

time: 32.9 us -> 27.7 us (0.84)
  local copies, waits for them, and re-layouts: 5.59 us -> 1.57 us
  Pallas kernels: 27 us -> 25.8 us
    unnamed x5 -> x1, local copies, waits for them, and re-layouts: 3.9 us -> 1.57 us
    pallas_call x1 -> x0, local copies, waits for them, and re-layouts: 1.69 us -> none  [by_rows(): pl.pallas_call(functools.partial(fused, tiles), out_shape=jax.ShapeDtypeS...]
    pallas_call x1, Pallas kernels: 27 us -> 25.8 us  [by_rows(): pl.pallas_call(functools.partial(fused, tiles), out_shape=jax.ShapeDtypeS...]
where the time goes in v2:
time: 27.7 us; the launch traced here: 27.4 us
  Pallas kernels  25.8 us (93%)
  local copies, waits for them, and re-layouts  1.57 us (6%)
    pallas_call x1, Pallas kernels, by_rows(): pl.pallas_call(functools.partial(fused, tiles), out_shape=jax.ShapeDtypeS...  25.8 us
    unnamed x1, local copies, waits for them, and re-layouts  1.57 us

profile of v2, /device:TPU:0, one launch (start us, length us, event | category | flops | bytes accessed | tf_op | source)
XLA Modules:
  0.0 27.4 jit_solution(1735473318703917867)
XLA Ops:
  0.0 25.8 %shard_map.46 = f32[1,8,32,48]{3,2,1,0:T(8,128)} custom-call(f32[1,8,32,48]{3,2,1,0:T(8,128)} %bitcast.5, s32[1,8,32,48]{3,2,1,0:T(8,128)} %bitcast.6, f32[9,1,32]{2,1,0:T(1,128)} %bitcast.7, s32[1,32]{1,0:T(1,128)} %shift_ref.1), custom_call_target="tpu_custom_call" | custom-call | tf_op jit(solution)/shard_map/pallas_call | solution.py:527
  25.9 1.6 %copy.6 = f32[1,8,48,32]{2,3,1,0:T(8,128)} copy(f32[1,8,48,32]{2,3,1,0:T(8,128)} %bitcast.4) | data formatting | bytes 98304

commit v3 on v2

--- a/solution.py
+++ b/solution.py
@@ -136,7 +136,92 @@
     return current[None]
 
 
-def fused(tiles, data_ref, labels_ref, taps_ref, shift_ref, out_ref, raw, raw_labels, taps_buf, shift_buf, mixed, packed, packed_labels, held, held_labels, mats, est, coef, outgoing, incoming, halo, back, unpacked, in_sem, send, recv, send_l, recv_l, send_m, recv_m, send_p, recv_p, send_h, recv_h, send_o, recv_o, out_sem):
+def gathered(parts, b_of, slot, depth):
+    fold = len(parts)
+    lanes = parts[0].shape[1]
+    total = None
+    for k in range(fold):
+        amount = (depth * (k - b_of[k])) % lanes
+        piece = pltpu.roll(parts[k], amount, 1) if amount else parts[k]
+        total = piece if total is None else jnp.where(slot == k, piece, total)
+    return total
+
+
+def turning(lanes, depth, flip_z):
+    row_ids = lax.broadcasted_iota(jnp.int32, (lanes, lanes), 0)
+    lane_ids = lax.broadcasted_iota(jnp.int32, (lanes, lanes), 1)
+    same_block = (row_ids // depth) == (lane_ids // depth)
+    aim = jnp.where(flip_z, depth - 1 - lane_ids % depth, lane_ids % depth)
+    return same_block, jnp.where(same_block & (row_ids % depth == aim), 1.0, 0.0).astype(jnp.float32)
+
+
+def exact(a, b):
+    return jnp.dot(a, b, precision=lax.Precision.HIGHEST, preferred_element_type=jnp.float32)
+
+
+def product(a, b, contract):
+    return lax.dot_general(a, b, (contract, ((), ())), preferred_element_type=jnp.float32)
+
+
+def halves(a):
+    high = a.astype(jnp.bfloat16)
+    return high, (a - high.astype(jnp.float32)).astype(jnp.bfloat16)
+
+
+def permuted(a, turn):
+    high, low = halves(a)
+    turn = turn.astype(jnp.bfloat16)
+    return product(high, turn, ((1,), (0,))) + product(low, turn, ((1,), (0,)))
+
+
+def blurred(a, matrix, contract):
+    high, low = halves(a)
+    return product(high, matrix[0], contract) + (
+        product(low, matrix[0], contract) + product(high, matrix[1], contract)
+    )
+
+
+def laid_out(back_ref, out_ref, back, mixed, unpacked, in_sem, out_sem):
+    copy = pltpu.make_async_copy(back_ref, back, in_sem)
+    copy.start()
+    slab, depth, rows = out_ref.shape[1:]
+    groups, _, lanes = back.shape
+    fold = lanes // depth
+    blocks = mixed.shape[0]
+    view = lax.axis_index("view")
+    flip_x = (view == 1) | (view == 2)
+    _, turn = turning(lanes, depth, view >= 2)
+    slot = lax.broadcasted_iota(jnp.int32, (mixed.shape[1] // fold, lanes), 1) // depth
+    copy.wait()
+    results = []
+    for j in range(blocks):
+        parts = []
+        for k in range(fold):
+            line = back[:, fold * j + k, :]
+            parts.append(
+                jnp.concatenate(
+                    [line, jnp.zeros((mixed.shape[1] // fold - groups, lanes), jnp.float32)], axis=0
+                )
+            )
+        for b in range(fold):
+            mixed[j, pl.ds(b, mixed.shape[1] // fold, stride=fold), :] = gathered(
+                parts, [b] * fold, slot, depth
+            )
+        unpacked[lanes * j : lanes * (j + 1), :] = permuted(mixed[j, 0:rows], turn).T
+        for k in range(fold):
+            x = fold * j + k
+            copy = pltpu.make_async_copy(
+                unpacked.at[pl.ds(x * depth, depth)],
+                out_ref.at[0, jnp.where(flip_x, slab - 1 - x, x)],
+                out_sem.at[x],
+            )
+            copy.start()
+            results.append(copy)
+    for copy in results:
+        copy.wait()
+
+
+def fused(tiles, data_ref, labels_ref, taps_ref, shift_ref, back, raw, raw_labels, taps_buf, shift_buf, mixed, packed, packed_labels, held, held_labels, mats, est, coef, outgoing, incoming, halo, in_sem, send, recv, send_l, recv_l, send_m, recv_m, send_p, recv_p, send_h, recv_h, send_o, recv_o):
     mesh_id = pl.DeviceIdType.MESH
     slab, depth, rows = data_ref.shape[1:]
     lanes = packed.shape[2]
@@ -181,40 +266,27 @@
         pl.semaphore_signal(barrier, inc=1, device_id=peer((me + d) % peers), device_id_type=mesh_id)
     pl.semaphore_signal(barrier, inc=1, device_id=across, device_id_type=mesh_id)
 
-    row_ids = lax.broadcasted_iota(jnp.int32, (lanes, lanes), 0)
-    lane_ids = lax.broadcasted_iota(jnp.int32, (lanes, lanes), 1)
-    same_block = (row_ids // depth) == (lane_ids // depth)
-    aim = jnp.where(flip_z, depth - 1 - lane_ids % depth, lane_ids % depth)
-    turn = jnp.where(same_block & (row_ids % depth == aim), 1.0, 0.0).astype(jnp.float32)
-
-    def exact(a, b):
-        return jnp.dot(a, b, precision=lax.Precision.HIGHEST, preferred_element_type=jnp.float32)
-
+    same_block, turn = turning(lanes, depth, flip_z)
     slot = lax.broadcasted_iota(jnp.int32, (mixed.shape[1] // fold, lanes), 1) // depth
     blocks = slab * depth // lanes
 
-    def gathered(parts, b_of):
-        total = None
-        for k in range(fold):
-            amount = (depth * (k - b_of[k])) % lanes
-            piece = pltpu.roll(parts[k], amount, 1) if amount else parts[k]
-            total = piece if total is None else jnp.where(slot == k, piece, total)
-        return total
-
-    def pack(source, target, fill, convert):
+    def pack(source, target, fill, turner):
         edge = jnp.full((1, slab, lanes), fill, jnp.float32)
         target[0:1] = edge
         target[groups + 1 : groups + 2] = edge
         for j in range(blocks):
-            block = convert(source[lanes * j : lanes * (j + 1), :])
-            mixed[j, 0:rows] = exact(block.T, turn)
+            mixed[j, 0:rows] = turner(source[lanes * j : lanes * (j + 1), :])
         for j in range(blocks):
             parts = [
                 mixed[j, pl.ds(b, mixed.shape[1] // fold, stride=fold), :] for b in range(fold)
             ]
             for k in range(fold):
-                line = gathered(parts, [k] * fold)
+                line = gathered(parts, [k] * fold, slot, depth)
                 target[1 : groups + 1, fold * j + k, :] = line[:groups]
+
+    def turned_labels(block):
+        block = block.astype(jnp.float32).T.astype(jnp.bfloat16)
+        return product(block, turn.astype(jnp.bfloat16), ((1,), (0,)))
 
     spot = pl.ds(pl.multiple_of(jnp.where(flip_x, tiles - 1 - tile, tile) * slab, 8), slab)
 
@@ -246,7 +318,7 @@
 
     for x in range(slab):
         copies_in[x].wait()
-    pack(raw, packed, 1.0, lambda v: v)
+    pack(raw, packed, 1.0, lambda v: permuted(v.T, turn))
     pl.semaphore_wait(barrier, peers)
     data_copies = scatter(packed, held, send, recv)
 
@@ -279,7 +351,7 @@
 
     for x in range(slab):
         copies_in[slab + x].wait()
-    pack(raw_labels, packed_labels, 0.0, lambda v: v.astype(jnp.float32))
+    pack(raw_labels, packed_labels, 0.0, turned_labels)
     label_copies = scatter(packed_labels, held_labels, send_l, recv_l)
 
     lane = lax.broadcasted_iota(jnp.int32, (cells, lanes), 1)
@@ -298,7 +370,7 @@
     def behind_y(fields, g):
         return jnp.where(
             first_lane,
-            pltpu.roll(fields[(g - 1) % width], depth, 1),
+            pltpu.roll(fields[g - 1], depth, 1),
             pltpu.roll(fields[g], depth, 1),
         )
 
@@ -321,7 +393,8 @@
     landed(data_copies)
     mat_copy.wait_recv()
     blurs = [
-        jnp.where(same_block, jnp.concatenate([mats[s]] * fold, axis=0), 0.0) for s in range(2)
+        halves(jnp.where(same_block, jnp.concatenate([mats[s]] * fold, axis=0), 0.0))
+        for s in range(2)
     ]
 
     def paired_of(step, chosen):
@@ -332,16 +405,8 @@
                 current = recorded
             else:
                 current = jnp.concatenate([est[s, g] for g in chosen], axis=0)
-            ratio = recorded / exact(current, blurs[s])
-            corrections.append(
-                lax.dot_general(
-                    ratio,
-                    blurs[s],
-                    (((1,), (1,)), ((), ())),
-                    precision=lax.Precision.HIGHEST,
-                    preferred_element_type=jnp.float32,
-                )
-            )
+            ratio = recorded / blurred(current, blurs[s], ((1,), (0,)))
+            corrections.append(blurred(ratio, blurs[s], ((1,), (1,))))
         return jnp.sqrt(corrections[0] * corrections[1])
 
     def swapped_over(step, number, begin, size):
@@ -357,6 +422,69 @@
         pending.append(copy)
         return copy
 
+    far = tile + 2 * role - 1
+    exists = (far >= 0) & (far < tiles)
+
+    def leaving(s, d, middle, relation):
+        t = (tile + d) % tiles
+        place = jnp.where(core == 1 - s, tiles - 1 - t, t)
+        here = 2 - role if middle else 1 + role
+        there = per_tile * tile + (1 if middle else 2 * role)
+        src = est.at[s, here, pl.ds(pl.multiple_of(place * slab, 8), slab), :]
+        if relation is None:
+            return pltpu.make_async_copy(src, back.at[there], recv_o.at[0, middle])
+        return pltpu.make_async_remote_copy(
+            src_ref=src,
+            dst_ref=back.at[there],
+            send_sem=send_o.at[s, 2 * d + middle],
+            recv_sem=recv_o.at[relation, 2 * d + middle],
+            device_id=(part, 2 * s + core, t),
+            device_id_type=mesh_id,
+        )
+
+    def arrived(d, middle, relation):
+        origin = (tile + tiles - d) % tiles
+        its_role = (half + relation + origin) % 2
+        there = per_tile * origin + (1 if middle else 2 * its_role)
+        pltpu.make_async_remote_copy(
+            src_ref=back.at[there],
+            dst_ref=back.at[there],
+            send_sem=send_o.at[0, 2 * d + middle],
+            recv_sem=recv_o.at[relation, 2 * d + middle],
+            device_id=across,
+            device_id_type=mesh_id,
+        ).wait_recv()
+
+    def send_back(s):
+        for d in range(1, tiles):
+            leaving(s, d, 0, (s + half) % 2).start()
+
+        @pl.when(half == 1 - s)
+        def _():
+            leaving(s, 0, 0, 1).start()
+
+        @pl.when(half == s)
+        def _():
+            for d in range(1, tiles):
+                leaving(s, d, 1, 0).start()
+            for middle in range(2):
+                leaving(s, 0, middle, None).start()
+
+    def sent_back(s):
+        for d in range(1, tiles):
+            leaving(s, d, 0, (s + half) % 2).wait_send()
+
+        @pl.when(half == 1 - s)
+        def _():
+            leaving(s, 0, 0, 1).wait_send()
+
+        @pl.when(half == s)
+        def _():
+            for d in range(1, tiles):
+                leaving(s, d, 1, 0).wait_send()
+            for middle in range(2):
+                leaving(s, 0, middle, None).wait()
+
     pending = []
     ready = {}
     for step in range(ITERS):
@@ -369,19 +497,18 @@
         else:
             inner = range(1, width - 1)
             outer = (0, width - 1)
-            near_copy, far_copy, exists = moving
             swaps = []
             for number, chosen in enumerate((inner, outer)):
                 if number:
-                    near_copy.wait()
                     near = (width - 1) * (1 - role)
                     for s in range(2):
+                        near_copies[s].wait()
                         est[s, pl.ds(near, 1)] = halo[step - 1, 1 - role, s][None]
 
                     @pl.when(exists)
                     def _():
-                        far_copy.wait()
                         for s in range(2):
+                            far_copies[s].wait()
                             est[s, pl.ds((width - 1) * role, 1)] = halo[step - 1, role, s][None]
 
                 part_p = paired_of(step, chosen)
@@ -410,13 +537,21 @@
         for swap in swaps:
             swap.wait_recv()
         joined = [jnp.sqrt(ready[g] * incoming[step, g]) for g in range(width)]
+        last = step == ITERS - 1
+        near_copies, far_copies = [], []
         for s in range(2):
             base = held if step == 0 else est
             fields = [base[s, g] * joined[g] for g in range(width)]
             for sweep in range(SWEEPS):
-                flux_y = [coef[2, s, g] * (ahead_y(fields, g) - fields[g]) for g in range(width)]
-                fresh = []
-                for g in range(width):
+                kept = range(1, width - 1) if sweep == SWEEPS - 1 else range(width)
+                flux_y = {
+                    g: coef[2, s, g] * (ahead_y(fields, g) - fields[g])
+                    for g in range(kept[0] - 1 if kept[0] else 0, kept[-1] + 1)
+                }
+                if kept[0] == 0:
+                    flux_y[-1] = flux_y[width - 1]
+                fresh = list(fields)
+                for g in kept:
                     f = fields[g]
                     flux_x = coef[0, s, g] * (pltpu.roll(f, cells - 1, 0) - f)
                     flux_z = coef[1, s, g] * (pltpu.roll(f, lanes - 1, 1) - f)
@@ -425,90 +560,41 @@
                         + (flux_y[g] - behind_y(flux_y, g))
                         + (flux_z - pltpu.roll(flux_z, 1, 1))
                     )
-                    fresh.append(f + total)
+                    fresh[g] = f + total
                 fields = fresh
             for g in range(width):
                 est[s, g] = fields[g]
-        if step < ITERS - 1:
-            far = tile + 2 * role - 1
-            exists = (far >= 0) & (far < tiles)
+            if last:
+                send_back(s)
+                continue
 
             def shifted(number, side, x_of, target):
                 return pltpu.make_async_remote_copy(
-                    src_ref=est.at[:, 1 + role],
-                    dst_ref=halo.at[step, side],
-                    send_sem=send_h.at[step, number],
-                    recv_sem=recv_h.at[step, number],
+                    src_ref=est.at[s, 1 + role],
+                    dst_ref=halo.at[step, side, s],
+                    send_sem=send_h.at[step, number, s],
+                    recv_sem=recv_h.at[step, number, s],
                     device_id=(part, 2 * x_of + core, target),
                     device_id_type=mesh_id,
                 )
 
-            near_copy = shifted(0, role, 1 - half, tile)
-            near_copy.start()
-            far_copy = shifted(1, 1 - role, half, jnp.clip(far, 0, tiles - 1))
+            near_copies.append(shifted(0, role, 1 - half, tile))
+            far_copies.append(shifted(1, 1 - role, half, jnp.clip(far, 0, tiles - 1)))
+            near_copies[s].start()
 
             @pl.when(exists)
             def _():
-                far_copy.start()
-
-            moving = (near_copy, far_copy, exists)
-
-    out_copies = []
-    for middle in range(2):
-        for d in range(tiles if middle else peers):
-            q = half * tiles + (tile + d) % tiles if middle else (me + d) % peers
-            s, t = q // tiles, q % tiles
-            place = jnp.where(s + core == 1, tiles - 1 - t, t)
-            here = 2 - role if middle else 1 + role
-            there = per_tile * tile + (1 if middle else 2 * role)
-            src = est.at[s, here, pl.ds(pl.multiple_of(place * slab, 8), slab), :]
-            dst = back.at[there]
-            number = peers * middle + d
-            if d == 0:
-                copy = pltpu.make_async_copy(src, dst, recv_o.at[number])
-            else:
-                copy = pltpu.make_async_remote_copy(
-                    src_ref=src,
-                    dst_ref=dst,
-                    send_sem=send_o.at[number],
-                    recv_sem=recv_o.at[number],
-                    device_id=peer(q),
-                    device_id_type=mesh_id,
-                )
-            copy.start()
-            out_copies.append(copy)
-    sent_out = []
-    for number, copy in enumerate(out_copies):
-        if number in (0, peers):
-            copy.wait()
-        else:
-            copy.wait_recv()
-            sent_out.append(copy)
-    for j in range(blocks):
-        parts = []
-        for k in range(fold):
-            line = back[:, fold * j + k, :]
-            parts.append(
-                jnp.concatenate(
-                    [line, jnp.zeros((mixed.shape[1] // fold - groups, lanes), jnp.float32)], axis=0
-                )
-            )
-        for b in range(fold):
-            mixed[j, pl.ds(b, mixed.shape[1] // fold, stride=fold), :] = gathered(parts, [b] * fold)
-    results = []
-    for j in range(blocks):
-        unpacked[lanes * j : lanes * (j + 1), :] = exact(mixed[j, 0:rows], turn).T
-    for x in range(slab):
-        at = jnp.where(flip_x, slab - 1 - x, x)
-        copy = pltpu.make_async_copy(
-            unpacked.at[pl.ds(pl.multiple_of(at * depth, 8), depth)], out_ref.at[0, x], out_sem.at[x]
-        )
-        copy.start()
-        results.append(copy)
-    for copy in data_copies[1:] + label_copies[1:] + [mat_copy] + pending + sent_out:
+                far_copies[s].start()
+
+    for d in range(tiles):
+        arrived(d, 0, 1)
+        if d:
+            arrived(d, 0, 0)
+            arrived(d, 1, 0)
+    for s in range(2):
+        sent_back(s)
+    for copy in data_copies[1:] + label_copies[1:] + [mat_copy] + pending:
         copy.wait_send()
-    for copy in results:
-        copy.wait()
 
 
 def by_rows(data, labels, kernel, offsets):
@@ -524,10 +610,10 @@
     wide = (2, width, cells, 128)
     dma = pltpu.SemaphoreType.DMA
     taps = kernel.transpose(2, 0, 1)
-    result = pl.pallas_call(
+    back = pl.pallas_call(
         functools.partial(fused, tiles),
-        out_shape=jax.ShapeDtypeStruct((1, slab, depth, rows), jnp.float32),
-        in_specs=[pl.BlockSpec(memory_space=pl.ANY)] * 4,
+        out_shape=jax.ShapeDtypeStruct((groups, slab, 128), jnp.float32),
+        in_specs=[pl.BlockSpec(memory_space=pltpu.HBM)] * 4,
         out_specs=pl.BlockSpec(memory_space=pl.ANY),
         scratch_shapes=[
             pltpu.VMEM(flat, jnp.float32),
@@ -545,8 +631,6 @@
             pltpu.VMEM((ITERS,) + wide[1:], jnp.float32),
             pltpu.VMEM((ITERS,) + wide[1:], jnp.float32),
             pltpu.VMEM((ITERS - 1, 2, 2, cells, 128), jnp.float32),
-            pltpu.VMEM((groups, slab, 128), jnp.float32),
-            pltpu.VMEM(flat, jnp.float32),
             dma((2 * slab + 2,)),
             dma((peers,)),
             dma((peers,)),
@@ -556,14 +640,28 @@
             dma(()),
             dma((ITERS, 3)),
             dma((ITERS, 3)),
-            dma((ITERS - 1, 2)),
-            dma((ITERS - 1, 2)),
-            dma((peers + tiles,)),
-            dma((peers + tiles,)),
+            dma((ITERS - 1, 2, 2)),
+            dma((ITERS - 1, 2, 2)),
+            dma((2, peers)),
+            dma((2, peers)),
+        ],
+        compiler_params=pltpu.CompilerParams(
+            collective_id=0, has_side_effects=True
+        ),
+    )(data.transpose(0, 1, 3, 2), labels.transpose(0, 1, 3, 2), taps, offsets)
+    result = pl.pallas_call(
+        laid_out,
+        out_shape=jax.ShapeDtypeStruct((1, slab, depth, rows), jnp.float32),
+        in_specs=[pl.BlockSpec(memory_space=pl.ANY)],
+        out_specs=pl.BlockSpec(memory_space=pltpu.HBM),
+        scratch_shapes=[
+            pltpu.VMEM((groups, slab, 128), jnp.float32),
+            pltpu.VMEM((slab * depth // 128, tall, 128), jnp.float32),
+            pltpu.VMEM(flat, jnp.float32),
+            dma(()),
             dma((slab,)),
         ],
-        compiler_params=pltpu.CompilerParams(collective_id=0, has_side_effects=True),
-    )(data.transpose(0, 1, 3, 2), labels.transpose(0, 1, 3, 2), taps, offsets)
+    )(back)
     return result.transpose(0, 1, 3, 2)
 
 

time: 27.7 us -> 26.5 us (0.957)
  local copies, waits for them, and re-layouts: 1.57 us -> 0 us
  Pallas kernels: 25.8 us -> 26.2 us
    pallas_call x0 -> x1, Pallas kernels: none -> 1.86 us  [by_rows(): pl.pallas_call(laid_out, out_shape=jax.ShapeDtypeStruct((1, slab, depth,...]
    unnamed x1 -> x0, local copies, waits for them, and re-layouts: 1.57 us -> none
    pallas_call x1, Pallas kernels: 25.8 us -> 24.4 us  [by_rows(): pl.pallas_call(functools.partial(fused, tiles), out_shape=jax.ShapeDtypeS...]
where the time goes in v3:
time: 26.5 us; the launch traced here: 26.2 us
  Pallas kernels  26.2 us (99%)
    pallas_call x1, Pallas kernels, by_rows(): pl.pallas_call(functools.partial(fused, tiles), out_shape=jax.ShapeDtypeS...  24.4 us
    pallas_call x1, Pallas kernels, by_rows(): pl.pallas_call(laid_out, out_shape=jax.ShapeDtypeStruct((1, slab, depth,...  1.86 us

profile of v3, /device:TPU:0, one launch (start us, length us, event | category | flops | bytes accessed | tf_op | source)
XLA Modules:
  0.0 26.2 jit_solution(16596437355705645191)
XLA Ops:
  0.0 24.4 %shard_map.46.back_ref = f32[12,8,128]{2,1,0:T(8,128)} custom-call(f32[1,8,32,48]{3,2,1,0:T(8,128)} %bitcast.4, s32[1,8,32,48]{3,2,1,0:T(8,128)} %bitcast.5, f32[9,1,32]{2,1,0:T(1,128)} %bitcast.6, s32[1,32]{1,0:T(1,128)} %shift_ref.1), custom_call_target="tpu_custom_call" | custom-call | tf_op jit(solution)/shard_map/pallas_call | solution.py:613
  24.4 1.9 %shard_map.47 = f32[1,8,32,48]{3,2,1,0:T(8,128)} custom-call(f32[12,8,128]{2,1,0:T(8,128)} %shard_map.46.back_ref), custom_call_target="tpu_custom_call" | custom-call | tf_op jit(solution)/shard_map/pallas_call | solution.py:652
